TPU v7x, 32 devices: a whole 2x2x4 slice. The times are simulated.
32 devices in a mesh: group: 4 (over y, x), shard: 8 (over z, core).
Axes of the slice: x: 2, y: 2, z: 4, core: 2. Of those that a mesh axis runs over, the one named last changes fastest.
Arguments:
- grad_pooled: bfloat16 [4096, 512, 128], P(('group', 'shard')), may hold values from -6 to 6
- bag_rows: int32 [4096, 512, 8], P(('group', 'shard')), may hold values from 0 to 511
- bag_lengths: int32 [4096, 512], P(('group', 'shard')), may hold values from 1 to 8
- table_order: int32 [512], replicated, may hold values from 0 to 511, each once
- weights: bfloat16 [512, 512, 128], P('shard'), may hold values from -6 to 6
- accum: float32 [512, 512], P('shard'), may hold values from 0.1 to 10
Outputs:
- new_weights: bfloat16 [512, 512, 128], P('shard')
- new_accum: float32 [512, 512], P('shard')
All inputs are finite; a program needn't handle non-finite values.
Results may differ from a plain program's by a relative error of at most 0.001.
Values may be sent and summed in bfloat16 or wider, within the bound.
A program may use at most 128 MiB of HBM per device.

v0:
```python
import functools

import jax
import jax.numpy as jnp
from jax import lax
from jax.experimental import pallas as pl
from jax.experimental.pallas import tpu as pltpu
from jax.sharding import PartitionSpec as P

LEARN_RATE = 0.5
EPSILON = 1e-06
AXES = ("group", "shard")
CHUNKS = 4
TILE = 16


def arrange_kernel(order_ref, grad_ref, *rest):
    *outs, flipped = rest
    tables = grad_ref.shape[1]
    part = outs[0].shape[0]

    def flip(step, carry):
        start = pl.multiple_of(step * TILE, TILE)
        block = grad_ref[:, pl.ds(start, TILE), :]
        flipped[pl.ds(start, TILE)] = jnp.swapaxes(block, 0, 1)
        return carry

    lax.fori_loop(0, tables // TILE, flip, 0)
    for chunk, out in enumerate(outs):

        def place(step, carry, chunk=chunk, out=out):
            for k in range(8):
                at = step * 8 + k
                out[at] = flipped[order_ref[chunk * part + at]]
            return carry

        lax.fori_loop(0, part // 8, place, 0)


def arrange(grad_pooled, order, chunks):
    samples, tables, width = grad_pooled.shape
    part = tables // chunks
    return pl.pallas_call(
        arrange_kernel,
        grid_spec=pltpu.PrefetchScalarGridSpec(
            num_scalar_prefetch=1,
            grid=(samples // TILE,),
            in_specs=[pl.BlockSpec((TILE, tables, width), lambda b, order: (b, 0, 0))],
            out_specs=[
                pl.BlockSpec((part, TILE, width), lambda b, order: (0, b, 0))
                for _ in range(chunks)
            ],
            scratch_shapes=[pltpu.VMEM((tables, TILE, width), grad_pooled.dtype)],
        ),
        out_shape=[
            jax.ShapeDtypeStruct((part, samples, width), grad_pooled.dtype)
            for _ in range(chunks)
        ],
        cost_estimate=pl.CostEstimate(
            flops=0, bytes_accessed=4 * grad_pooled.size, transcendentals=0
        ),
    )(order, grad_pooled)


def expand_kernel(offset, unroll, rows_ref, grad_ref, out_ref, counts):
    sources, _, bag, samples = rows_ref.shape
    row_count = out_ref.shape[1]
    place = lax.broadcasted_iota(jnp.int32, (TILE, samples), 0).astype(jnp.float32)
    places = [(place + float(r * TILE - offset)).astype(jnp.bfloat16) for r in range(row_count // TILE)]
    one = jnp.ones((TILE, samples), jnp.bfloat16)
    zero = jnp.zeros((TILE, samples), jnp.bfloat16)
    out_ref[...] = jnp.zeros_like(out_ref)

    def step(i, carry):
        for u in range(unroll):
            picks = rows_ref[i * unroll + u, 0].astype(jnp.float32)
            spread = [
                jnp.broadcast_to(picks[j : j + 1], (TILE, samples)).astype(jnp.bfloat16)
                for j in range(bag)
            ]
            for r, here in enumerate(places):
                terms = [jnp.where(s == here, one, zero) for s in spread]
                while len(terms) > 1:
                    terms = [a + b for a, b in zip(terms[::2], terms[1::2])] + (
                        [terms[-1]] if len(terms) % 2 else []
                    )
                counts[r * TILE : (r + 1) * TILE, u * samples : (u + 1) * samples] = terms[0]
        values = grad_ref[pl.ds(i * unroll, unroll), 0].reshape(unroll * samples, -1)
        out_ref[0] += jnp.dot(counts[...], values, preferred_element_type=jnp.float32)
        return carry

    lax.fori_loop(0, sources // unroll, step, 0)


def expand_rows(gradient, row_ids, first, row_count, offset):
    sources, tables, samples, width = gradient.shape
    bag = row_ids.shape[2]
    unroll = 4 if sources % 4 == 0 else 1
    return pl.pallas_call(
        functools.partial(expand_kernel, offset, unroll),
        grid=(tables,),
        in_specs=[
            pl.BlockSpec((sources, 1, bag, samples), lambda t: (0, first + t, 0, 0)),
            pl.BlockSpec((sources, 1, samples, width), lambda t: (0, t, 0, 0)),
        ],
        out_specs=pl.BlockSpec((1, row_count, width), lambda t: (t, 0, 0)),
        out_shape=jax.ShapeDtypeStruct((tables, row_count, width), jnp.float32),
        scratch_shapes=[pltpu.VMEM((row_count, unroll * samples), jnp.bfloat16)],
        cost_estimate=pl.CostEstimate(
            flops=40 * gradient.size * row_count // 8,
            bytes_accessed=2 * gradient.size,
            transcendentals=0,
        ),
    )(row_ids, gradient)


def body(grad_pooled, bag_rows, bag_lengths, table_order, weights, accum):
    row_count = weights.shape[1]
    samples, tables, width = grad_pooled.shape
    bag = bag_rows.shape[2]
    groups = lax.axis_size("group")
    shards = lax.axis_size("shard")
    devices = groups * shards
    held = weights.shape[0]
    quarter = held // groups
    chunks = CHUNKS if quarter % CHUNKS == 0 else 1
    each = quarter // chunks
    offset = row_count // 2
    me = lax.axis_index("group")

    by_slot = table_order.reshape(shards, chunks, groups, each)
    by_chunk = by_slot.transpose(1, 2, 0, 3).reshape(-1)
    by_device = by_slot.transpose(2, 0, 1, 3).reshape(-1)

    live = jnp.arange(bag, dtype=jnp.int32)[None, :, None] < bag_lengths[:, None, :]
    ids = jnp.where(live, jnp.transpose(bag_rows, (0, 2, 1)), row_count) - offset
    ids = jnp.transpose(ids.astype(jnp.float32), (2, 1, 0))
    ids = jnp.take(ids, by_device, axis=0, mode="clip", unique_indices=True).astype(jnp.bfloat16)
    ids = lax.all_to_all(ids, AXES, split_axis=0, concat_axis=0, tiled=True)
    ids = ids.reshape(devices, quarter, bag, samples)

    sends = arrange(grad_pooled, by_chunk, chunks)
    received = []
    for chunk in range(chunks):
        send = sends[chunk]
        if received:
            send, received[-1] = lax.optimization_barrier((send, received[-1]))
        received.append(lax.all_to_all(send, AXES, split_axis=0, concat_axis=0, tiled=True))

    weights_by = weights.reshape(chunks, groups, each, row_count, width)
    accum_by = accum.reshape(chunks, groups, each, row_count)
    full_weights, sums = [], []
    for chunk in range(chunks):
        gradient = received[chunk].reshape(devices, each, samples, width)
        row_grad = expand_rows(gradient, ids, chunk * each, row_count, offset)
        weight_part = lax.dynamic_index_in_dim(weights_by[chunk], me, 0, keepdims=False)
        accum_part = lax.dynamic_index_in_dim(accum_by[chunk], me, 0, keepdims=False)
        new_accum = accum_part + jnp.mean(row_grad * row_grad, axis=-1)
        step_size = LEARN_RATE / (jnp.sqrt(new_accum) + EPSILON)
        new_weights = weight_part.astype(jnp.float32) - step_size[:, :, None] * row_grad
        full_weights.append(
            lax.all_gather(new_weights.astype(jnp.bfloat16), "group", axis=0, tiled=True)
        )
        sums.append(new_accum)
    all_sums = lax.all_gather(jnp.stack(sums), "group", axis=1)
    return (
        jnp.concatenate(full_weights, axis=0),
        all_sums.reshape(held, row_count),
    )


def solution(mesh):
    in_specs = (
        P(AXES, None, None),
        P(AXES, None, None),
        P(AXES, None),
        P(),
        P("shard", None, None),
        P("shard", None),
    )
    out_specs = (P("shard", None, None), P("shard", None))
    return jax.shard_map(body, mesh=mesh, in_specs=in_specs, out_specs=out_specs, check_vma=False)
```

profile of v0, /device:TPU:0, one launch (start us, length us, event | category | flops | bytes accessed | tf_op | source)
XLA Modules:
  0.0 532.7 jit_solution(918405155562617016)
XLA Ops:
  7.2 0.8 reshape.137
  8.0 0.7 reshape.139.order_ref
  8.7 20.4 %shard_map.77 = (bf16[128,128,128]{2,1,0:T(8,128)(2,1)}, bf16[128,128,128]{2,1,0:T(8,128)(2,1)}, bf16[128,128,128]{2,1,0:T(8,128)(2,1)}, bf16[128,128,128]{2,1,0:T(8,128)(2,1)}) custom-call(s32[512]{0:T(512)} %reshape.139.order_ref, bf16[128,512,128]{2,1,0:T(8,128)(2,1)} %grad_ref.1), custom_call_target="tpu_custom_call" | custom-call | bytes 33554432 | tf_op jit(solution)/shard_map/pallas_call | solution.py:43
  29.1 102.3 %all_to_all.25 = bf16[128,128,128]{2,1,0:T(8,128)(2,1)} all-to-all(bf16[128,128,128]{2,1,0:T(8,128)(2,1)} %get-tuple-element.13), channel_id=1, replica_groups=mesh['group'=4,'shard'=8] {'group','shard'}, dimensions={0} | all-to-all | bytes 8388608 | tf_op jit(solution)/shard_map/all_to_all | solution.py:148
  131.4 3.6 all-to-all-start.2
  135.0 0.1 reshape.151
  135.2 0.0 copy-start.1
  135.2 2.3 copy.21
  137.5 0.0 copy-done.1
  137.5 0.1 copy.20
  137.7 0.3 fusion.1
  138.0 2.4 gather_fusion
  140.4 89.6 %all-to-all-done.2 = bf16[128,128,128]{2,1,0:T(8,128)(2,1)} async-done(((bf16[128,128,128]{2,1,0:T(8,128)(2,1)}), bf16[128,128,128]{2,1,0:T(8,128)(2,1)}, u32[]{:S(2)}, u32[]{:S(2)}) %all-to-all-start.2) | async-done | bytes 4194336 | tf_op jit(solution)/shard_map/all_to_all | solution.py:148
  230.0 2.6 all-to-all-start
  232.6 0.0 copy-start.2
  232.6 27.5 %all-to-all-done = bf16[512,8,128]{2,1,0:T(8,128)(2,1)S(1)} async-done(((bf16[512,8,128]{2,1,0:T(8,128)(2,1)}), bf16[512,8,128]{2,1,0:T(8,128)(2,1)S(1)}, u32[]{:S(2)}, u32[]{:S(2)}) %all-to-all-start) | async-done | bytes 1048608 | tf_op jit(solution)/shard_map/all_to_all | solution.py:139
  260.1 0.0 copy-start
  260.1 1.1 copy-done
  261.2 3.6 all-to-all-start.3
  264.7 0.0 all-gather.6.cloned.1.call-start
  264.8 0.0 copy-done.2
  264.9 5.7 %fusion.18 = (bf16[16,512,128]{2,1,0:T(8,128)(2,1)}, bf16[16,512,128]{2,1,0:T(8,128)(2,1)}, bf16[16,512,128]{2,1,0:T(8,128)(2,1)S(1)}, bf16[16,512,128]{2,1,0:T(8,128)(2,1)}) fusion(bf16[64,512,128]{2,1,0:T(8,128)(2,1)} %param.10), kind=kLoop, calls=%fused_computation.40 | loop fusion | bytes 16777216 | tf_op jit(solution)/shard_map/slice | solution.py:156
  270.6 23.9 %shard_map.78 = f32[4,512,128]{2,1,0:T(8,128)} custom-call(bf16[32,16,8,128]{3,2,1,0:T(8,128)(2,1)} %bitcast.78, bf16[32,4,128,128]{3,2,1,0:T(8,128)(2,1)} %bitcast.73), custom_call_target="tpu_custom_call" | custom-call | flops 5368709120 | bytes 4194304 | tf_op jit(solution)/shard_map/pallas_call | solution.py:99
  294.5 1.6 multiply_reduce_fusion.3
  296.1 2.5 fusion.5
  298.6 0.0 all-gather.6.cloned.1.call-update
  298.6 61.1 %all-to-all-done.3 = bf16[128,128,128]{2,1,0:T(8,128)(2,1)} async-done(((bf16[128,128,128]{2,1,0:T(8,128)(2,1)}), bf16[128,128,128]{2,1,0:T(8,128)(2,1)}, u32[]{:S(2)}, u32[]{:S(2)}) %all-to-all-start.3) | async-done | bytes 4194336 | tf_op jit(solution)/shard_map/all_to_all | solution.py:148
  359.7 3.6 all-to-all-start.4
  363.3 0.0 all-gather.8.cloned.1.call-start
  363.3 23.9 %shard_map.79 = f32[4,512,128]{2,1,0:T(8,128)} custom-call(bf16[32,16,8,128]{3,2,1,0:T(8,128)(2,1)} %bitcast.79, bf16[32,4,128,128]{3,2,1,0:T(8,128)(2,1)} %bitcast.12.grad_ref), custom_call_target="tpu_custom_call" | custom-call | flops 5368709120 | bytes 4194304 | tf_op jit(solution)/shard_map/pallas_call | solution.py:99
  387.2 1.6 multiply_reduce_fusion.2
  388.9 2.5 fusion.4
  391.4 0.0 all-gather.8.cloned.1.call-update
  391.4 0.0 all-gather.10.cloned.1.call-start
  391.5 23.9 %shard_map.80 = f32[4,512,128]{2,1,0:T(8,128)} custom-call(bf16[32,16,8,128]{3,2,1,0:T(8,128)(2,1)} %bitcast.80, bf16[32,4,128,128]{3,2,1,0:T(8,128)(2,1)} %bitcast.16.grad_ref), custom_call_target="tpu_custom_call" | custom-call | flops 5368709120 | bytes 4194304 | tf_op jit(solution)/shard_map/pallas_call | solution.py:99
  415.4 1.6 multiply_reduce_fusion.1
  417.0 2.5 fusion.3
  419.5 0.0 all-gather.10.cloned.1.call-update
  419.5 0.0 all-gather.12.cloned.1.call-start
  419.6 38.8 %all-to-all-done.4 = bf16[128,128,128]{2,1,0:T(8,128)(2,1)} async-done(((bf16[128,128,128]{2,1,0:T(8,128)(2,1)}), bf16[128,128,128]{2,1,0:T(8,128)(2,1)}, u32[]{:S(2)}, u32[]{:S(2)}) %all-to-all-start.4) | async-done | bytes 4194336 | tf_op jit(solution)/shard_map/all_to_all | solution.py:148
  458.3 23.9 %shard_map.81 = f32[4,512,128]{2,1,0:T(8,128)} custom-call(bf16[32,16,8,128]{3,2,1,0:T(8,128)(2,1)} %bitcast.81, bf16[32,4,128,128]{3,2,1,0:T(8,128)(2,1)} %bitcast.20.grad_ref), custom_call_target="tpu_custom_call" | custom-call | flops 5368709120 | bytes 4194304 | tf_op jit(solution)/shard_map/pallas_call | solution.py:99
  482.2 1.6 multiply_reduce_fusion
  483.8 2.4 fusion.2
  486.2 0.0 all-gather.12.cloned.1.call-update
  486.3 7.5 %all-gather = f32[4,16,512]{2,0,1:T(4,128)S(1)} all-gather(f32[4,4,512]{2,0,1:T(4,128)S(1)} %copy.24), channel_id=2, replica_groups=mesh['group'=4,'shard'=8] {'group'}, dimensions={1}, use_global_device_ids=true | all-gather | bytes 163840 | tf_op jit(solution)/shard_map/all_gather | solution.py:165
  493.8 0.7 copy.25
  494.5 24.4 %all-gather.12.cloned.1.call-done = bf16[16,512,128]{2,1,0:T(8,128)(2,1)} async-done(((bf16[4,512,128]{2,1,0:T(8,128)(2,1)}), bf16[16,512,128]{2,1,0:T(8,128)(2,1)}) %all-gather.12.cloned.1.call-update) | async-done | bytes 2097168 | tf_op jit(solution)/shard_map/all_gather | solution.py:162
  519.0 7.2 %pad_maximum_fusion = bf16[64,512,128]{2,1,0:T(8,128)(2,1)} fusion(bf16[16,512,128]{2,1,0:T(8,128)(2,1)} %all-gather.12.cloned.1.call-done, bf16[16,512,128]{2,1,0:T(8,128)(2,1)} %all-gather.10.cloned.1.call-done, bf16[16,512,128]{2,1,0:T(8,128)(2,1)} %all-gather.8.cloned.1.call-done, bf16[16,512,128]{2,1,0:T(8,128)(2,1)} %all-gather.6.cloned.1.call-done), kind=kLoop, calls=%fused_computation.1 | loop fusion | flops 12582912 | bytes 16777216 | tf_op jit(solution)/shard_map/concatenate | solution.py:167
  (19 shorter events, 0.3 us)
Async XLA Ops:
  131.4 98.5 %all-to-all-start.2 = ((bf16[128,128,128]{2,1,0:T(8,128)(2,1)}), bf16[128,128,128]{2,1,0:T(8,128)(2,1)}, u32[]{:S(2)}, u32[]{:S(2)}) async-start(bf16[128,128,128]{2,1,0:T(8,128)(2,1)} %get-tuple-element.16), calls=%async_computation.2 | async-start | bytes 8388608 | tf_op jit(solution)/shard_map/all_to_all | solution.py:148
  135.2 2.4 copy-start.1
  230.0 30.1 %all-to-all-start = ((bf16[512,8,128]{2,1,0:T(8,128)(2,1)}), bf16[512,8,128]{2,1,0:T(8,128)(2,1)S(1)}, u32[]{:S(2)}, u32[]{:S(2)}) async-start(bf16[512,8,128]{2,1,0:T(8,128)(2,1)} %gather_fusion), calls=%async_computation | async-start | bytes 2097152 | tf_op jit(solution)/shard_map/all_to_all | solution.py:139
  232.6 32.2 %copy-start.2 = (f32[64,512]{1,0:T(8,128)S(1)}, f32[64,512]{1,0:T(8,128)}, u32[]{:S(2)}) copy-start(f32[64,512]{1,0:T(8,128)} %param.11) | copy-start | bytes 393220
  260.1 1.1 copy-start
  261.2 98.5 %all-to-all-start.3 = ((bf16[128,128,128]{2,1,0:T(8,128)(2,1)}), bf16[128,128,128]{2,1,0:T(8,128)(2,1)}, u32[]{:S(2)}, u32[]{:S(2)}) async-start(bf16[128,128,128]{2,1,0:T(8,128)(2,1)} %get-tuple-element.19), calls=%async_computation.3 | async-start | bytes 8388608 | tf_op jit(solution)/shard_map/all_to_all | solution.py:148
  264.7 229.8 %all-gather.6.cloned.1.call-start = ((), (), s32[]{:S(2)}) async-start(), calls=%async_computation.5 | async-start | bytes 2621440 | tf_op jit(solution)/shard_map/all_gather | solution.py:162
  359.7 98.6 %all-to-all-start.4 = ((bf16[128,128,128]{2,1,0:T(8,128)(2,1)}), bf16[128,128,128]{2,1,0:T(8,128)(2,1)}, u32[]{:S(2)}, u32[]{:S(2)}) async-start(bf16[128,128,128]{2,1,0:T(8,128)(2,1)} %get-tuple-element.21), calls=%async_computation.4 | async-start | bytes 8388608 | tf_op jit(solution)/shard_map/all_to_all | solution.py:148
  363.3 131.3 %all-gather.8.cloned.1.call-start = ((), (), s32[]{:S(2)}) async-start(), calls=%async_computation.6 | async-start | bytes 2621440 | tf_op jit(solution)/shard_map/all_gather | solution.py:162
  391.4 103.2 %all-gather.10.cloned.1.call-start = ((), (), s32[]{:S(2)}) async-start(), calls=%async_computation.7 | async-start | bytes 2621440 | tf_op jit(solution)/shard_map/all_gather | solution.py:162
  419.5 99.5 %all-gather.12.cloned.1.call-start = ((), (), s32[]{:S(2)}) async-start(), calls=%async_computation.8 | async-start | bytes 2621440 | tf_op jit(solution)/shard_map/all_gather | solution.py:162
Sparse Core Ops, SparseCore 0:
  298.8 43.7 all-gather.5
  391.5 48.1 all-gather.7
  441.5 35.5 all-gather.9
  486.4 32.5 all-gather.11
where the time goes:
time: 534 us; the launch traced here: 533 us
  waiting for transfers between devices  241 us (45%)
  Pallas kernels  116 us (22%)
  blocking collectives  110 us (21%)
  other arithmetic  23.9 us (4%)
  local copies, waits for them, and re-layouts  14.1 us (3%)
  between operations  14 us (3%)
  starting transfers between devices  13.6 us (3%)
    all_to_all x3, waiting for transfers between devices, body(): lax.all_to_all(send, AXES, split_axis=0, concat_axis=0, tiled=True)  189 us
    all_to_all x1, blocking collectives, body(): lax.all_to_all(send, AXES, split_axis=0, concat_axis=0, tiled=True)  102 us
    pallas_call x4, Pallas kernels, expand_rows(): pl.pallas_call(functools.partial(expand_kernel, offset, unroll), grid=(ta...  95.6 us
    all_to_all x1, waiting for transfers between devices, body(): ids = lax.all_to_all(ids, AXES, split_axis=0, concat_axis=0, tiled=True)  27.5 us
    all_gather x4, waiting for transfers between devices, body(): lax.all_gather(new_weights.astype(jnp.bfloat16), 'group', axis=0, tiled=T...  24.4 us
    pallas_call x1, Pallas kernels, arrange(): pl.pallas_call(arrange_kernel, grid_spec=pltpu.PrefetchScalarGridSpec(num...  20.4 us
    all_to_all x3, starting transfers between devices, body(): lax.all_to_all(send, AXES, split_axis=0, concat_axis=0, tiled=True)  10.7 us
  transfers between devices with their start and end apart: 8, of which 5 were waited for; matrix products, arithmetic and copies ran while one was open for 5% of the time, Pallas kernels for 18%

commit v1 on v0

v1 whole, which is shorter than its diff:
```python
import functools

import jax
import jax.numpy as jnp
from jax import lax
from jax.experimental import pallas as pl
from jax.experimental.pallas import tpu as pltpu
from jax.sharding import PartitionSpec as P

LEARN_RATE = 0.5
EPSILON = 1e-06
AXES = ("group", "shard")
TILE = 16
STEPS_AHEAD = 6
LEVELS = 32760.0
SMALLEST = 1e-30
MESH = pl.DeviceIdType.MESH


def arrange_kernel(order_ref, grad_ref, out_ref, flipped):
    tables = grad_ref.shape[1]

    def flip(step, carry):
        start = pl.multiple_of(step * TILE, TILE)
        block = grad_ref[:, pl.ds(start, TILE), :]
        flipped[pl.ds(start, TILE)] = jnp.swapaxes(block, 0, 1)
        return carry

    lax.fori_loop(0, tables // TILE, flip, 0)

    def place(step, carry):
        for k in range(8):
            at = step * 8 + k
            out_ref[at] = flipped[order_ref[at]]
        return carry

    lax.fori_loop(0, tables // 8, place, 0)


def arrange(grad_pooled, order):
    samples, tables, width = grad_pooled.shape
    return pl.pallas_call(
        arrange_kernel,
        grid_spec=pltpu.PrefetchScalarGridSpec(
            num_scalar_prefetch=1,
            grid=(samples // TILE,),
            in_specs=[pl.BlockSpec((TILE, tables, width), lambda b, order: (b, 0, 0))],
            out_specs=pl.BlockSpec((tables, TILE, width), lambda b, order: (0, b, 0)),
            scratch_shapes=[pltpu.VMEM((tables, TILE, width), grad_pooled.dtype)],
        ),
        out_shape=jax.ShapeDtypeStruct((tables, samples, width), grad_pooled.dtype),
        cost_estimate=pl.CostEstimate(
            flops=0, bytes_accessed=4 * grad_pooled.size, transcendentals=0
        ),
    )(order, grad_pooled)


def sum_rows(load_ids, load_values, sources, counts, acc, offset):
    row_count, wide = counts.shape
    bag, samples = load_ids(0).shape
    unroll = wide // samples
    place = lax.broadcasted_iota(jnp.int32, (TILE, samples), 0).astype(jnp.float32)
    places = [(place + float(r * TILE - offset)).astype(jnp.bfloat16) for r in range(row_count // TILE)]
    one = jnp.ones((TILE, samples), jnp.bfloat16)
    zero = jnp.zeros((TILE, samples), jnp.bfloat16)
    for turn in range(sources // unroll):
        for u in range(unroll):
            picks = load_ids(turn * unroll + u).astype(jnp.float32)
            spread = [
                jnp.broadcast_to(picks[j : j + 1], (TILE, samples)).astype(jnp.bfloat16)
                for j in range(bag)
            ]
            for r, here in enumerate(places):
                terms = [jnp.where(s == here, one, zero) for s in spread]
                while len(terms) > 1:
                    terms = [a + b for a, b in zip(terms[::2], terms[1::2])] + (
                        [terms[-1]] if len(terms) % 2 else []
                    )
                counts[r * TILE : (r + 1) * TILE, u * samples : (u + 1) * samples] = terms[0]
        values = load_values(turn * unroll, unroll)
        part = lax.dot_general(
            values, counts[...], (((0,), (1,)), ((), ())), preferred_element_type=jnp.float32
        )
        if turn == 0:
            acc[...] = part
        else:
            acc[...] += part


def exchange_kernel(
    cores, lines, offset,
    sends, ids, weights, accum, new_weights, new_accum,
    raw, raw_ids, counts, acc, parts, scales, got_parts, got_scales, own,
    held_weights, held_accum, made_weights, made_accum,
    raw_sent, raw_got, ids_sent, ids_got, local,
    parts_sent, parts_got, scales_sent, scales_got,
    weights_sent, weights_got, accum_sent, accum_got,
):
    steps, plane, batch = sends.shape[:3]
    groups = plane // cores
    rounds = steps // lines
    ahead = raw_sent.shape[0]
    bag, samples = ids.shape[-2:]
    width, row_count = acc.shape
    g = lax.axis_index("group")
    s = lax.axis_index("shard")
    z, c = s // cores, s % cores
    p = g * cores + c

    def in_plane(o):
        q = (p + o) % plane
        return q, (q // cores, z * cores + q % cores)

    def in_line(d):
        far = (z + 1 + d) % lines
        return far, (g, far * cores + c)

    barrier = pltpu.get_barrier_semaphore()
    for o in range(1, plane):
        pl.semaphore_signal(barrier, inc=1, device_id=in_plane(o)[1], device_id_type=MESH)
    for d in range(lines - 1):
        pl.semaphore_signal(barrier, inc=1, device_id=in_line(d)[1], device_id_type=MESH)

    locals_ = [
        pltpu.make_async_copy(sends.at[:, p], raw.at[:, p], local.at[0]),
        pltpu.make_async_copy(ids.at[p], raw_ids.at[p], local.at[1]),
        pltpu.make_async_copy(weights.at[g], held_weights, local.at[2]),
        pltpu.make_async_copy(accum.at[g], held_accum, local.at[3]),
    ]
    for copy in locals_:
        copy.start()
    pl.semaphore_wait(barrier, plane - 1 + lines - 1)

    for o in range(1, plane):
        q, device = in_plane(o)
        pltpu.make_async_remote_copy(
            src_ref=ids.at[q], dst_ref=raw_ids.at[p], send_sem=ids_sent, recv_sem=ids_got,
            device_id=device, device_id_type=MESH,
        ).start()

    def place_of(n):
        return in_line(n % lines)[0] * rounds + n // lines

    def send_raw(n):
        a = place_of(n)
        for o in range(1, plane):
            q, device = in_plane(o)
            pltpu.make_async_remote_copy(
                src_ref=sends.at[a, q], dst_ref=raw.at[a, p],
                send_sem=raw_sent.at[n % ahead], recv_sem=raw_got.at[a],
                device_id=device, device_id_type=MESH,
            ).start()

    def wait_bytes(ref, sem):
        pltpu.make_async_copy(ref, ref, sem).wait()

    def first(n, carry):
        send_raw(n)
        return carry

    lax.fori_loop(0, ahead, first, 0)
    for copy in locals_:
        copy.wait()
    wait_bytes(raw_ids.at[pl.ds(0, plane - 1)], ids_got)

    def finish(i):
        for d in range(lines - 1):
            wait_bytes(got_parts.at[i, d], parts_got.at[i, d])
            wait_bytes(got_scales.at[i, d], scales_got.at[i, d])

        def table(kk, carry):
            at = i * batch + kk
            total = own[at]
            for d in range(lines - 1):
                far = got_parts[i, d, kk].astype(jnp.int32).astype(jnp.float32)
                total += far * got_scales[i, d, kk, 0:1, :]
            square = jnp.sum(total * total, axis=0, keepdims=True) * (1.0 / width)
            sums = held_accum[pl.ds(at, 1), :] + square
            made_accum[pl.ds(at, 1), :] = sums
            step_size = LEARN_RATE / (jnp.sqrt(sums) + EPSILON)
            change = (total * step_size).T
            made_weights[at] = (held_weights[at].astype(jnp.float32) - change).astype(jnp.bfloat16)
            return carry

        lax.fori_loop(0, batch, table, 0)
        mine = pl.ds(i * batch, batch)
        for o in range(1, groups):
            pltpu.make_async_remote_copy(
                src_ref=made_weights.at[mine], dst_ref=new_weights.at[g, mine],
                send_sem=weights_sent, recv_sem=weights_got.at[o - 1],
                device_id=((g + o) % groups, s), device_id_type=MESH,
            ).start()
        pltpu.make_async_copy(made_weights.at[mine], new_weights.at[g, mine], local.at[4]).start()

    def step(n, carry):
        i, d = n // lines, n % lines
        a = place_of(n)

        @pl.when(n + ahead < steps)
        def _():
            wait_bytes(raw.at[a, pl.ds(0, plane - 1)], raw_sent.at[n % ahead])
            send_raw(n + ahead)

        wait_bytes(raw.at[a, pl.ds(0, plane - 1)], raw_got.at[a])

        def table(kk, carry):
            sum_rows(
                lambda b: raw_ids[b, a, kk],
                lambda b, many: raw[a, b : b + many, kk].reshape(many * samples, width),
                plane, counts, acc, offset,
            )

            @pl.when(d < lines - 1)
            def _():
                value = acc[...]
                top = jnp.maximum(jnp.max(jnp.abs(value), axis=0, keepdims=True), SMALLEST)
                coded = jnp.round(value * (LEVELS / top))
                parts[i, d, kk] = coded.astype(jnp.int32).astype(jnp.int16)
                scales[i, d, kk] = jnp.broadcast_to(top * (1.0 / LEVELS), (8, row_count))

            @pl.when(d == lines - 1)
            def _():
                own[i * batch + kk] = acc[...]

            return carry

        lax.fori_loop(0, batch, table, 0)

        @pl.when(d < lines - 1)
        def _():
            device = in_line(d)[1]
            pltpu.make_async_remote_copy(
                src_ref=parts.at[i, d], dst_ref=got_parts.at[i, d],
                send_sem=parts_sent, recv_sem=parts_got.at[i, d],
                device_id=device, device_id_type=MESH,
            ).start()
            pltpu.make_async_remote_copy(
                src_ref=scales.at[i, d], dst_ref=got_scales.at[i, d],
                send_sem=scales_sent, recv_sem=scales_got.at[i, d],
                device_id=device, device_id_type=MESH,
            ).start()

        @pl.when((d == lines - 1) & (i > 0))
        def _():
            finish(i - 1)

        return carry

    lax.fori_loop(0, steps, step, 0)
    finish(rounds - 1)

    for o in range(1, groups):
        pltpu.make_async_remote_copy(
            src_ref=made_accum, dst_ref=new_accum.at[g],
            send_sem=accum_sent, recv_sem=accum_got.at[o - 1],
            device_id=((g + o) % groups, s), device_id_type=MESH,
        ).start()
    last = pltpu.make_async_copy(made_accum, new_accum.at[g], local.at[5])
    last.start()

    def drain(n, carry):
        wait_bytes(raw.at[0, pl.ds(0, plane - 1)], raw_sent.at[n])
        return carry

    lax.fori_loop(0, ahead, drain, 0)
    wait_bytes(raw_ids.at[pl.ds(0, plane - 1)], ids_sent)
    wait_bytes(parts, parts_sent)
    wait_bytes(scales, scales_sent)
    wait_bytes(new_weights.at[g], local.at[4])
    last.wait()
    wait_bytes(new_weights.at[pl.ds(0, groups - 1)], weights_sent)
    wait_bytes(new_accum.at[pl.ds(0, groups - 1)], accum_sent)
    for o in range(1, groups):
        wait_bytes(new_weights.at[g], weights_got.at[o - 1])
        wait_bytes(new_accum.at[g], accum_got.at[o - 1])


def exchange(sends, ids, weights, accum, cores, lines, offset):
    steps, plane, batch, samples, width = sends.shape
    groups, quarter, row_count, _ = weights.shape
    bag = ids.shape[-2]
    rounds = steps // lines
    ahead = min(STEPS_AHEAD, steps)
    far = max(lines - 1, 1)
    unroll = 4 if plane % 4 == 0 else 1
    dma = pltpu.SemaphoreType.DMA
    anywhere = pl.BlockSpec(memory_space=pl.ANY)
    return pl.pallas_call(
        functools.partial(exchange_kernel, cores, lines, offset),
        in_specs=[anywhere] * 4,
        out_specs=[anywhere] * 2,
        out_shape=[
            jax.ShapeDtypeStruct(weights.shape, weights.dtype),
            jax.ShapeDtypeStruct(accum.shape, accum.dtype),
        ],
        scratch_shapes=[
            pltpu.VMEM((steps, plane, batch, samples, width), sends.dtype),
            pltpu.VMEM((plane, steps, batch, bag, samples), ids.dtype),
            pltpu.VMEM((row_count, unroll * samples), jnp.bfloat16),
            pltpu.VMEM((width, row_count), jnp.float32),
            pltpu.VMEM((rounds, far, batch, width, row_count), jnp.int16),
            pltpu.VMEM((rounds, far, batch, 8, row_count), jnp.float32),
            pltpu.VMEM((rounds, far, batch, width, row_count), jnp.int16),
            pltpu.VMEM((rounds, far, batch, 8, row_count), jnp.float32),
            pltpu.VMEM((quarter, width, row_count), jnp.float32),
            pltpu.VMEM((quarter, row_count, width), weights.dtype),
            pltpu.VMEM((quarter, row_count), jnp.float32),
            pltpu.VMEM((quarter, row_count, width), weights.dtype),
            pltpu.VMEM((quarter, row_count), jnp.float32),
            dma((ahead,)), dma((steps,)), dma, dma, dma((6,)),
            dma, dma((rounds, far)), dma, dma((rounds, far)),
            dma, dma((groups - 1,)), dma, dma((groups - 1,)),
        ],
        compiler_params=pltpu.CompilerParams(
            collective_id=0, has_side_effects=True, vmem_limit_bytes=60 * 2**20
        ),
    )(sends, ids, weights, accum)


def body(grad_pooled, bag_rows, bag_lengths, table_order, weights, accum):
    held, row_count, width = weights.shape
    samples, tables, _ = grad_pooled.shape
    bag = bag_rows.shape[2]
    groups = lax.axis_size("group")
    shards = lax.axis_size("shard")
    cores = 2 if shards % 2 == 0 else 1
    lines = shards // cores
    plane = groups * cores
    quarter = held // groups
    batch = 2 if quarter % 2 == 0 else 1
    rounds = quarter // batch
    steps = lines * rounds
    offset = row_count // 2

    by_slot = table_order.reshape(lines, cores, groups, rounds, batch)
    by_step = by_slot.transpose(0, 3, 2, 1, 4).reshape(-1)
    by_device = by_slot.transpose(2, 1, 0, 3, 4).reshape(-1)

    live = jnp.arange(bag, dtype=jnp.int32)[None, :, None] < bag_lengths[:, None, :]
    ids = jnp.where(live, jnp.transpose(bag_rows, (0, 2, 1)), row_count) - offset
    ids = jnp.transpose(ids.astype(jnp.float32), (2, 1, 0))
    ids = jnp.take(ids, by_device, axis=0, mode="clip", unique_indices=True).astype(jnp.bfloat16)
    ids = ids.reshape(plane, steps, batch, bag, samples)

    sends = arrange(grad_pooled, by_step).reshape(steps, plane, batch, samples, width)
    new_weights, new_accum = exchange(
        sends, ids,
        weights.reshape(groups, quarter, row_count, width),
        accum.reshape(groups, quarter, row_count),
        cores, lines, offset,
    )
    return new_weights.reshape(weights.shape), new_accum.reshape(accum.shape)


def solution(mesh):
    in_specs = (
        P(AXES, None, None),
        P(AXES, None, None),
        P(AXES, None),
        P(),
        P("shard", None, None),
        P("shard", None),
    )
    out_specs = (P("shard", None, None), P("shard", None))
    return jax.shard_map(body, mesh=mesh, in_specs=in_specs, out_specs=out_specs, check_vma=False)
```

time: 534 us -> 329 us (0.62)
  waiting for transfers between devices: 241 us -> 0 us
  Pallas kernels: 116 us -> 312 us
  blocking collectives: 110 us -> 0 us
  other arithmetic: 23.9 us -> 0.35 us
  starting transfers between devices: 13.6 us -> 0 us
  between operations: 14 us -> 0.7 us
    all_to_all x4 -> x0, waiting for transfers between devices: 217 us -> none  [the longest x3 189 us: body(): lax.all_to_all(send, AXES, split_axis=0, concat_axis=0, tiled=True)]
    pallas_call x4 -> x1, Pallas kernels: 95.6 us -> 292 us  [exchange(): pl.pallas_call(functools.partial(exchange_kernel, cores, lines, offset),...]
    all_to_all x1 -> x0, blocking collectives: 102 us -> none  [body(): lax.all_to_all(send, AXES, split_axis=0, concat_axis=0, tiled=True)]
    all_gather x4 -> x0, waiting for transfers between devices: 24.4 us -> none  [body(): lax.all_gather(new_weights.astype(jnp.bfloat16), 'group', axis=0, tiled=T...]
    all_to_all x4 -> x0, starting transfers between devices: 13.4 us -> none  [the longest x3 10.7 us: body(): lax.all_to_all(send, AXES, split_axis=0, concat_axis=0, tiled=True)]
    convert_element_type x4 -> x0, other arithmetic: 9.92 us -> none  [body(): new_weights.astype(jnp.bfloat16)]
    all_gather x1 -> x0, blocking collectives: 7.52 us -> none  [body(): all_sums = lax.all_gather(jnp.stack(sums), 'group', axis=1)]
    unnamed x7 -> x5, local copies, waits for them, and re-layouts: 3.41 us -> 10.8 us
  transfers between devices with their start and end apart: 8 -> 0, of which waited for: 5 -> 0; matrix products, arithmetic and copies ran while one was open for 5% -> 0% of each run, Pallas kernels for 18% -> 0%
where the time goes in v1:
time: 329 us
  Pallas kernels  312 us (95%)
  local copies, waits for them, and re-layouts  16 us (5%)
    pallas_call x1, Pallas kernels, exchange(): pl.pallas_call(functools.partial(exchange_kernel, cores, lines, offset),...  292 us
    pallas_call x1, Pallas kernels, arrange(): pl.pallas_call(arrange_kernel, grid_spec=pltpu.PrefetchScalarGridSpec(num...  20.4 us
    unnamed x5, local copies, waits for them, and re-layouts  10.8 us

profile of v1, /device:TPU:0, one launch (start us, length us, event | category | flops | bytes accessed | tf_op | source)
XLA Modules:
  0.0 329.0 jit_solution(12777719841335348125)
XLA Ops:
  0.6 0.8 reshape.31
  1.5 0.1 copy.9
  1.6 0.8 reshape.32.order_ref
  2.3 0.1 reshape.40
  2.5 1.1 copy.10
  3.6 2.3 copy.11
  5.9 0.3 fusion.1
  6.2 2.4 gather_fusion
  8.6 20.4 %shard_map.77 = bf16[512,128,128]{2,1,0:T(8,128)(2,1)} custom-call(s32[512]{0:T(512)} %reshape.32.order_ref, bf16[128,512,128]{2,1,0:T(8,128)(2,1)} %grad_ref.1), custom_call_target="tpu_custom_call" | custom-call | bytes 33554432 | tf_op jit(solution)/shard_map/pallas_call | solution.py:42
  29.0 291.5 %shard_map.78 = (bf16[4,16,512,128]{3,2,1,0:T(8,128)(2,1)}, f32[4,16,512]{2,1,0:T(8,128)}) custom-call(bf16[32,8,2,128,128]{4,3,2,1,0:T(8,128)(2,1)} %bitcast.17, bf16[8,32,2,8,128]{4,3,2,1,0:T(8,128)(2,1)} %bitcast.20, bf16[4,16,512,128]{3,2,1,0:T(8,128)(2,1)} %bitcast.18, f32[4,16,512]{2,1,0:T(8,128)} %bitcast.24), custom_call_target="tpu_custom_call" | custom-call | tf_op jit(solution)/shard_map/pallas_call | solution.py:288
  320.5 0.0 copy-start
  320.5 7.8 %copy.15 = bf16[64,512,128]{2,1,0:T(8,128)(2,1)} copy(bf16[64,512,128]{2,1,0:T(8,128)(2,1)} %bitcast.19) | data formatting | bytes 16777216
  328.4 0.0 copy-done
  328.4 0.7 copy.16
  (2 shorter events, 0.0 us)
Async XLA Ops:
  320.5 7.8 %copy-start = (f32[4,16,512]{2,1,0:T(8,128)S(1)}, f32[4,16,512]{2,1,0:T(8,128)}, u32[]{:S(2)}) copy-start(f32[4,16,512]{2,1,0:T(8,128)} %get-tuple-element.5) | copy-start | bytes 393220

commit v2 on v1

v2 whole, which is shorter than its diff:
```python
import functools

import jax
import jax.numpy as jnp
import numpy as np
from jax import lax
from jax.experimental import pallas as pl
from jax.experimental.pallas import tpu as pltpu
from jax.sharding import PartitionSpec as P

LEARN_RATE = 0.5
EPSILON = 1e-06
AXES = ("group", "shard")
TILE = 16
BLOCK = 32
STEPS_AHEAD = 8
PASS_AFTER = 4
FINISH_AFTER = 0
SPAN = 4
LEVELS = 32760.0
SMALLEST = 1e-30
MESH = pl.DeviceIdType.MESH


def arrange_kernel(place_ref, grad_ref, out_ref):
    tables = grad_ref.shape[1]

    def flip(step, carry):
        start = pl.multiple_of(step * TILE, TILE)
        block = jnp.swapaxes(grad_ref[:, pl.ds(start, TILE), :], 0, 1)
        for k in range(TILE):
            out_ref[place_ref[start + k]] = block[k]
        return carry

    lax.fori_loop(0, tables // TILE, flip, 0)


def arrange(grad_pooled, places):
    samples, tables, width = grad_pooled.shape
    block = BLOCK if samples % BLOCK == 0 else TILE
    return pl.pallas_call(
        arrange_kernel,
        grid_spec=pltpu.PrefetchScalarGridSpec(
            num_scalar_prefetch=1,
            grid=(samples // block,),
            in_specs=[pl.BlockSpec((block, tables, width), lambda b, places: (b, 0, 0))],
            out_specs=pl.BlockSpec((tables, block, width), lambda b, places: (0, b, 0)),
        ),
        out_shape=jax.ShapeDtypeStruct((tables, samples, width), grad_pooled.dtype),
        cost_estimate=pl.CostEstimate(
            flops=0, bytes_accessed=4 * grad_pooled.size, transcendentals=0
        ),
    )(places, grad_pooled)


def sum_rows(load_ids, load_values, sources, counts, acc, offset):
    row_count, wide = counts.shape
    bag, samples = load_ids(0).shape
    unroll = wide // samples
    place = lax.broadcasted_iota(jnp.int32, (TILE, samples), 0).astype(jnp.float32)
    places = [(place + float(r * TILE - offset)).astype(jnp.bfloat16) for r in range(row_count // TILE)]
    one = jnp.ones((TILE, samples), jnp.bfloat16)
    zero = jnp.zeros((TILE, samples), jnp.bfloat16)
    for turn in range(sources // unroll):
        for u in range(unroll):
            picks = load_ids(turn * unroll + u).astype(jnp.float32)
            spread = [
                jnp.broadcast_to(picks[j : j + 1], (TILE, samples)).astype(jnp.bfloat16)
                for j in range(bag)
            ]
            for r, here in enumerate(places):
                terms = [jnp.where(s == here, one, zero) for s in spread]
                while len(terms) > 1:
                    terms = [a + b for a, b in zip(terms[::2], terms[1::2])] + (
                        [terms[-1]] if len(terms) % 2 else []
                    )
                counts[r * TILE : (r + 1) * TILE, u * samples : (u + 1) * samples] = terms[0]
        values = load_values(turn * unroll, unroll)
        part = lax.dot_general(
            values, counts[...], (((0,), (1,)), ((), ())), preferred_element_type=jnp.float32
        )
        if turn == 0:
            acc[...] = part
        else:
            acc[...] += part


class Split:
    def __init__(self, groups, shards):
        self.cores = 2 if shards % 2 == 0 else 1
        self.low = 2 if groups % 2 == 0 else 1
        self.near = 2 if (shards // self.cores) % 2 == 0 else 1
        self.groups = groups
        self.lines = shards // self.cores
        self.plane = groups * self.cores
        self.square = groups == 4 and self.low == 2
        self.mixed = self.square and self.near == 2
        self.span = SPAN if self.mixed else 1

    def turn(self, n, rounds):
        full = rounds // self.span * self.span
        block = self.span * self.lines
        if full == 0:
            return n % rounds, n // rounds
        short = n // (full * self.lines)
        many = self.span + (rounds - full - self.span) * short
        at = n - n // block * block
        return n // block * self.span + at % many, at // many

    def masks(self, i):
        if not self.mixed:
            return 1, 0, 0
        m = (i % 2) * (1 + i % 4 // 2)
        return (m - 1) * (m - 2) // 2, m * (2 - m), m * (m - 1) // 2

    def here(self, i, g, s):
        flat, swap_high, swap_low = self.masks(i)
        z, c = s // self.cores, s % self.cores
        high, low = g // self.low, g % self.low
        far, near = z // self.near, z % self.near
        first = high * (1 - swap_high) + near * swap_high
        second = low * (1 - swap_low) + near * swap_low
        rest = near * flat + high * swap_high + low * swap_low
        return (first * self.low + second) * self.cores + c, far * self.near + rest

    def device(self, i, p, line):
        flat, swap_high, swap_low = self.masks(i)
        c, pair = p % self.cores, p // self.cores
        first, second = pair // self.low, pair % self.low
        far, rest = line // self.near, line % self.near
        high = first * (1 - swap_high) + rest * swap_high
        low = second * (1 - swap_low) + rest * swap_low
        near = rest * flat + first * swap_high + second * swap_low
        return high * self.low + low, (far * self.near + near) * self.cores + c


def exchange_kernel(
    split, offset,
    sends, ids, weights, accum, new_weights, new_accum,
    raw, raw_ids, counts, acc, parts, scales, got_parts, got_scales, own,
    held_weights, held_accum, made_weights, made_accum,
    raw_sent, raw_got, raw_kept, ids_sent, ids_got, ids_kept, local,
    parts_sent, parts_got, scales_sent, scales_got,
    weights_sent, weights_got, passed_got, accum_sent, accum_got,
):
    steps, plane, batch = sends.shape[:3]
    groups, lines = split.groups, split.lines
    rounds = steps // lines
    ahead = raw_sent.shape[0]
    block = split.span * lines
    width, row_count = acc.shape
    g = lax.axis_index("group")
    s = lax.axis_index("shard")
    z = s // split.cores

    def remote(src, dst, sent, got, device):
        return pltpu.make_async_remote_copy(
            src_ref=src, dst_ref=dst, send_sem=sent, recv_sem=got,
            device_id=device, device_id_type=MESH,
        )

    def wait_bytes(ref, sem):
        pltpu.make_async_copy(ref, ref, sem).wait()

    barrier = pltpu.get_barrier_semaphore()
    greeted = 0
    for kind in (0, 1, 3) if split.mixed else (0,):
        p, line = split.here(kind, g, s)
        for o in range(1, plane):
            pl.semaphore_signal(
                barrier, inc=1, device_id=split.device(kind, (p + o) % plane, line),
                device_id_type=MESH,
            )
        for d in range(lines - 1):
            pl.semaphore_signal(
                barrier, inc=1, device_id=split.device(kind, p, (line + 1 + d) % lines),
                device_id_type=MESH,
            )
        greeted += plane - 1 + lines - 1

    held = [
        pltpu.make_async_copy(weights.at[g], held_weights, local.at[0]),
        pltpu.make_async_copy(accum.at[g], held_accum, local.at[1]),
    ]
    for copy in held:
        copy.start()
    pl.semaphore_wait(barrier, greeted)

    def place_of(n):
        i, d = split.turn(n, rounds)
        p, line = split.here(i, g, s)
        return i, d, p, line, (line + 1 + d) % lines

    def send_raw(n):
        i, d, p, line, to = place_of(n)

        @pl.when(d == 0)
        def _():
            for o in range(1, plane):
                q = (p + o) % plane
                remote(
                    ids.at[i, :, q], raw_ids.at[i, :, p], ids_sent, ids_got.at[i],
                    split.device(i, q, line),
                ).start()
            pltpu.make_async_copy(ids.at[i, :, p], raw_ids.at[i, :, p], ids_kept.at[i]).start()

        a = i * lines + to
        for o in range(1, plane):
            q = (p + o) % plane
            remote(
                sends.at[a, q], raw.at[a, p], raw_sent.at[n % ahead], raw_got.at[a],
                split.device(i, q, line),
            ).start()
        pltpu.make_async_copy(sends.at[a, p], raw.at[a, p], raw_kept.at[n % ahead]).start()

    def first(n, carry):
        send_raw(n)
        return carry

    lax.fori_loop(0, ahead, first, 0)
    for copy in held:
        copy.wait()
    others = pl.ds(0, plane - 1)
    beside = (g // split.low) * split.low + (g % split.low + 1) % split.low
    across = (g + split.low) % groups
    half = row_count // 2

    def finish(i):
        for d in range(lines - 1):
            wait_bytes(got_parts.at[i, d], parts_got.at[i, d])
            wait_bytes(got_scales.at[i, d], scales_got.at[i, d])

        def table(kk, carry):
            at = i * batch + kk
            total = own[at]
            for d in range(lines - 1):
                far = got_parts[i, d, kk].astype(jnp.int32).astype(jnp.float32)
                total += far * got_scales[i, d, pl.ds(kk, 1), :]
            square = jnp.sum(total * total, axis=0, keepdims=True) * (1.0 / width)
            sums = held_accum[pl.ds(at, 1), :] + square
            made_accum[pl.ds(at, 1), :] = sums
            step_size = LEARN_RATE / (jnp.sqrt(sums) + EPSILON)
            change = (total * step_size).T
            made_weights[at] = (held_weights[at].astype(jnp.float32) - change).astype(jnp.bfloat16)
            return carry

        lax.fori_loop(0, batch, table, 0)
        mine = pl.ds(i * batch, batch)
        if split.square:
            targets = [beside, across]
        else:
            targets = [(g + o) % groups for o in range(1, groups)]
        for at, to in enumerate(targets):
            remote(
                made_weights.at[mine], new_weights.at[g, mine],
                weights_sent, weights_got.at[i, at], (to, s),
            ).start()
        pltpu.make_async_copy(made_weights.at[mine], new_weights.at[g, mine], local.at[2]).start()

    def pass_on(i):
        if not split.square:
            return
        mine = pl.ds(i * batch, batch)
        for at, (source, to) in enumerate(((beside, across), (across, beside))):
            wait_bytes(new_weights.at[source, mine], weights_got.at[i, at])
            rows = new_weights.at[source, mine, pl.ds(at * half, half)]
            remote(rows, rows, weights_sent, passed_got.at[at], (to, s)).start()

    def step(n, carry):
        i, d, p, line, to = place_of(n)
        a = i * lines + to

        wait_bytes(raw.at[a, p], raw_kept.at[n % ahead])

        @pl.when(n + ahead < steps)
        def _():
            wait_bytes(raw.at[a, others], raw_sent.at[n % ahead])
            send_raw(n + ahead)

        @pl.when(d == 0)
        def _():
            wait_bytes(raw_ids.at[i, :, p], ids_kept.at[i])
            wait_bytes(raw_ids.at[i, :, others], ids_got.at[i])

        wait_bytes(raw.at[a, others], raw_got.at[a])

        def table(kk, carry):
            sum_rows(
                lambda b: raw_ids[i, to, b, kk],
                lambda b, many: raw[a, b : b + many, kk].reshape(many * samples, width),
                plane, counts, acc, offset,
            )

            @pl.when(d < lines - 1)
            def _():
                value = acc[...]
                top = jnp.maximum(jnp.max(jnp.abs(value), axis=0, keepdims=True), SMALLEST)
                coded = jnp.round(value * (LEVELS / top))
                parts[i, d, kk] = coded.astype(jnp.int32).astype(jnp.int16)
                scales[i, d, pl.ds(kk, 1), :] = top * (1.0 / LEVELS)

            @pl.when(d == lines - 1)
            def _():
                own[i * batch + kk] = acc[...]

            return carry

        samples = raw.shape[3]
        lax.fori_loop(0, batch, table, 0)

        @pl.when(d < lines - 1)
        def _():
            device = split.device(i, p, to)
            remote(
                parts.at[i, d], got_parts.at[i, d], parts_sent, parts_got.at[i, d], device
            ).start()
            remote(
                scales.at[i, d], got_scales.at[i, d], scales_sent, scales_got.at[i, d], device
            ).start()

        back = n - block - FINISH_AFTER
        done = back // block * split.span

        @pl.when((back >= 0) & (back % block < split.span))
        def _():
            finish(done + back % block)

        later = back - PASS_AFTER

        @pl.when((later >= 0) & (later % block < split.span))
        def _():
            pass_on(later // block * split.span + later % block)

        return carry

    lax.fori_loop(0, steps, step, 0)
    due = [i // split.span * block + block + i % split.span + FINISH_AFTER for i in range(rounds)]
    for i in range(rounds):
        if due[i] >= steps:
            finish(i)
        elif due[i] + PASS_AFTER >= steps:
            pass_on(i)

    for o in range(1, groups):
        remote(
            made_accum, new_accum.at[g], accum_sent, accum_got.at[o - 1], ((g + o) % groups, s)
        ).start()
    last = pltpu.make_async_copy(made_accum, new_accum.at[g], local.at[3])
    last.start()
    for i in range(rounds):
        if due[i] >= steps:
            pass_on(i)

    def drain(n, carry):
        wait_bytes(raw.at[0, others], raw_sent.at[n])
        return carry

    lax.fori_loop(0, ahead, drain, 0)
    wait_bytes(raw_ids.at[:, :, others], ids_sent)
    wait_bytes(parts, parts_sent)
    wait_bytes(scales, scales_sent)
    wait_bytes(new_weights.at[g], local.at[2])
    last.wait()
    wait_bytes(new_weights.at[pl.ds(0, groups - 1)], weights_sent)
    wait_bytes(new_accum.at[pl.ds(0, groups - 1)], accum_sent)
    for o in range(1, groups):
        wait_bytes(new_accum.at[g], accum_got.at[o - 1])
    if split.square:
        for at in range(2):
            wait_bytes(new_weights.at[g, :, pl.ds(0, half)], passed_got.at[at])
    else:
        for i in range(rounds):
            for o in range(1, groups):
                wait_bytes(new_weights.at[g, pl.ds(i * batch, batch)], weights_got.at[i, o - 1])


def exchange(sends, ids, weights, accum, split, offset):
    steps, plane, batch, samples, width = sends.shape
    groups, quarter, row_count, _ = weights.shape
    bag = ids.shape[-2]
    lines = split.lines
    rounds = steps // lines
    ahead = min(STEPS_AHEAD, steps)
    far = max(lines - 1, 1)
    unroll = 4 if plane % 4 == 0 else 1
    dma = pltpu.SemaphoreType.DMA
    anywhere = pl.BlockSpec(memory_space=pl.ANY)
    return pl.pallas_call(
        functools.partial(exchange_kernel, split, offset),
        in_specs=[anywhere] * 4,
        out_specs=[anywhere] * 2,
        out_shape=[
            jax.ShapeDtypeStruct(weights.shape, weights.dtype),
            jax.ShapeDtypeStruct(accum.shape, accum.dtype),
        ],
        scratch_shapes=[
            pltpu.VMEM((steps, plane, batch, samples, width), sends.dtype),
            pltpu.VMEM((rounds, lines, plane, batch, bag, samples), ids.dtype),
            pltpu.VMEM((row_count, unroll * samples), jnp.bfloat16),
            pltpu.VMEM((width, row_count), jnp.float32),
            pltpu.VMEM((rounds, far, batch, width, row_count), jnp.int16),
            pltpu.VMEM((rounds, far, 8, row_count), jnp.float32),
            pltpu.VMEM((rounds, far, batch, width, row_count), jnp.int16),
            pltpu.VMEM((rounds, far, 8, row_count), jnp.float32),
            pltpu.VMEM((quarter, width, row_count), jnp.float32),
            pltpu.VMEM((quarter, row_count, width), weights.dtype),
            pltpu.VMEM((quarter, row_count), jnp.float32),
            pltpu.VMEM((quarter, row_count, width), weights.dtype),
            pltpu.VMEM((quarter, row_count), jnp.float32),
            dma((ahead,)), dma((steps,)), dma((ahead,)), dma, dma((rounds,)), dma((rounds,)),
            dma((4,)),
            dma, dma((rounds, far)), dma, dma((rounds, far)),
            dma, dma((rounds, groups - 1)), dma((2,)), dma, dma((groups - 1,)),
        ],
        compiler_params=pltpu.CompilerParams(
            collective_id=0, has_side_effects=True, vmem_limit_bytes=60 * 2**20
        ),
    )(sends, ids, weights, accum)


def body(grad_pooled, bag_rows, bag_lengths, table_order, weights, accum):
    held, row_count, width = weights.shape
    samples, tables, _ = grad_pooled.shape
    bag = bag_rows.shape[2]
    split = Split(lax.axis_size("group"), lax.axis_size("shard"))
    groups, lines, plane = split.groups, split.lines, split.plane
    quarter = held // groups
    batch = 2 if quarter % 32 == 0 else 1
    rounds = quarter // batch
    steps = lines * rounds
    offset = row_count // 2

    i, line, p, k = np.meshgrid(*map(np.arange, (rounds, lines, plane, batch)), indexing="ij")
    group, shard = split.device(i, p, line)
    slots = (shard * held + group * quarter + i * batch + k).reshape(-1)
    numbers = np.arange(tables)
    from_slot = jnp.asarray(slots[:, None] == numbers[None, :])
    order = jnp.sum(jnp.where(from_slot, table_order[None, :], 0), axis=1)
    at_slot = jnp.asarray(np.argsort(slots), jnp.int32)
    table_at = table_order[None, :] == jnp.arange(tables, dtype=jnp.int32)[:, None]
    places = jnp.sum(jnp.where(table_at, at_slot[None, :], 0), axis=1)

    live = jnp.arange(bag, dtype=jnp.int32)[None, :, None] < bag_lengths[:, None, :]
    ids = jnp.where(live, jnp.transpose(bag_rows, (0, 2, 1)), row_count) - offset
    ids = jnp.transpose(ids.astype(jnp.float32), (2, 1, 0))
    ids = jnp.take(ids, order, axis=0, mode="clip", unique_indices=True).astype(jnp.bfloat16)
    ids = ids.reshape(rounds, lines, plane, batch, bag, samples)

    sends = arrange(grad_pooled, places).reshape(steps, plane, batch, samples, width)
    new_weights, new_accum = exchange(
        sends, ids,
        weights.reshape(groups, quarter, row_count, width),
        accum.reshape(groups, quarter, row_count),
        split, offset,
    )
    return new_weights.reshape(weights.shape), new_accum.reshape(accum.shape)


def solution(mesh):
    in_specs = (
        P(AXES, None, None),
        P(AXES, None, None),
        P(AXES, None),
        P(),
        P("shard", None, None),
        P("shard", None),
    )
    out_specs = (P("shard", None, None), P("shard", None))
    return jax.shard_map(body, mesh=mesh, in_specs=in_specs, out_specs=out_specs, check_vma=False)
```

time: 329 us -> 286 us (0.87)
  Pallas kernels: 312 us -> 269 us
    pallas_call x1, Pallas kernels: 292 us -> 254 us  [exchange(): pl.pallas_call(functools.partial(exchange_kernel, split, offset), in_spec...]
    pallas_call x1, Pallas kernels: 20.4 us -> 15.2 us  [arrange(): pl.pallas_call(arrange_kernel, grid_spec=pltpu.PrefetchScalarGridSpec(num...]
where the time goes in v2:
time: 286 us
  Pallas kernels  269 us (94%)
  local copies, waits for them, and re-layouts  14.2 us (5%)
    pallas_call x1, Pallas kernels, exchange(): pl.pallas_call(functools.partial(exchange_kernel, split, offset), in_spec...  254 us
    pallas_call x1, Pallas kernels, arrange(): pl.pallas_call(arrange_kernel, grid_spec=pltpu.PrefetchScalarGridSpec(num...  15.2 us
    unnamed x5, local copies, waits for them, and re-layouts  10.8 us

profile of v2, /device:TPU:0, one launch (start us, length us, event | category | flops | bytes accessed | tf_op | source)
XLA Modules:
  0.0 286.1 jit_solution(1906633383759793937)
XLA Ops:
  0.6 1.9 select_reduce_fusion
  2.5 1.1 copy.13
  3.6 2.3 copy.14
  5.9 0.3 fusion.1
  6.2 2.4 gather_fusion
  8.6 15.2 %shard_map.95 = bf16[512,128,128]{2,1,0:T(8,128)(2,1)} custom-call(s32[512]{0:T(512)} %get-tuple-element.7.place_ref, bf16[128,512,128]{2,1,0:T(8,128)(2,1)} %grad_ref.1), custom_call_target="tpu_custom_call" | custom-call | bytes 33554432 | tf_op jit(solution)/shard_map/pallas_call | solution.py:41
  23.8 253.8 %shard_map.96 = (bf16[4,16,512,128]{3,2,1,0:T(8,128)(2,1)}, f32[4,16,512]{2,1,0:T(8,128)}) custom-call(bf16[64,8,1,128,128]{4,3,2,1,0:T(8,128)(2,1)} %bitcast.13, bf16[16,4,8,1,8,128]{5,4,3,2,1,0:T(8,128)(2,1)} %bitcast.16, bf16[4,16,512,128]{3,2,1,0:T(8,128)(2,1)} %bitcast.14, f32[4,16,512]{2,1,0:T(8,128)} %bitcast.18), custom_call_target="tpu_custom_call" | custom-call | tf_op jit(solution)/shard_map/pallas_call | solution.py:388
  277.6 0.0 copy-start
  277.6 7.8 %copy.18 = bf16[64,512,128]{2,1,0:T(8,128)(2,1)} copy(bf16[64,512,128]{2,1,0:T(8,128)(2,1)} %bitcast.15) | data formatting | bytes 16777216
  285.4 0.0 copy-done
  285.4 0.7 copy.19
  (1 shorter events, 0.0 us)
Async XLA Ops:
  277.6 7.8 %copy-start = (f32[4,16,512]{2,1,0:T(8,128)S(1)}, f32[4,16,512]{2,1,0:T(8,128)}, u32[]{:S(2)}) copy-start(f32[4,16,512]{2,1,0:T(8,128)} %get-tuple-element.5) | copy-start | bytes 393220

commit v3 on v2

--- a/solution.py
+++ b/solution.py
@@ -15,7 +15,8 @@
 BLOCK = 32
 STEPS_AHEAD = 8
 PASS_AFTER = 4
-FINISH_AFTER = 0
+NARROW = 2
+NARROW_ROUNDS = 4
 SPAN = 4
 LEVELS = 32760.0
 SMALLEST = 1e-30
@@ -97,15 +98,27 @@
         self.mixed = self.square and self.near == 2
         self.span = SPAN if self.mixed else 1
 
+    def spans(self, rounds):
+        wide = max(rounds - NARROW_ROUNDS, 0) // self.span * self.span
+        narrow = NARROW if self.mixed and (rounds - wide) % NARROW == 0 else 1
+        return wide, narrow
+
     def turn(self, n, rounds):
-        full = rounds // self.span * self.span
-        block = self.span * self.lines
-        if full == 0:
-            return n % rounds, n // rounds
-        short = n // (full * self.lines)
-        many = self.span + (rounds - full - self.span) * short
-        at = n - n // block * block
-        return n // block * self.span + at % many, at // many
+        wide, narrow = self.spans(rounds)
+        steps = rounds * self.lines
+        if wide == 0:
+            late, many, at = 1, narrow, n
+        else:
+            late = (n + steps - wide * self.lines) // steps
+            many = self.span + (narrow - self.span) * late
+            at = n - wide * self.lines * late
+        block = many * self.lines
+        return wide * late + at // block * many + at % many, at % block // many
+
+    def due(self, i, rounds):
+        wide, narrow = self.spans(rounds)
+        base, many = (0, self.span) if i < wide else (wide, narrow)
+        return (base + (i - base) // many * many + many) * self.lines + (i - base) % many
 
     def masks(self, i):
         if not self.mixed:
@@ -136,10 +149,10 @@
 
 def exchange_kernel(
     split, offset,
-    sends, ids, weights, accum, new_weights, new_accum,
-    raw, raw_ids, counts, acc, parts, scales, got_parts, got_scales, own,
-    held_weights, held_accum, made_weights, made_accum,
-    raw_sent, raw_got, raw_kept, ids_sent, ids_got, ids_kept, local,
+    order, sends, bag_rows, bag_lengths, weights, accum, new_weights, new_accum,
+    raw, raw_ids, rows, lengths, by_table, ids, counts, acc, parts, scales, got_parts, got_scales, own,
+    held_weights, held_accum, made_accum,
+    raw_sent, raw_got, raw_kept, ids_sent, ids_got, local,
     parts_sent, parts_got, scales_sent, scales_got,
     weights_sent, weights_got, passed_got, accum_sent, accum_got,
 ):
@@ -147,7 +160,7 @@
     groups, lines = split.groups, split.lines
     rounds = steps // lines
     ahead = raw_sent.shape[0]
-    block = split.span * lines
+    wide, narrow = split.spans(rounds)
     width, row_count = acc.shape
     g = lax.axis_index("group")
     s = lax.axis_index("shard")
@@ -181,6 +194,8 @@
     held = [
         pltpu.make_async_copy(weights.at[g], held_weights, local.at[0]),
         pltpu.make_async_copy(accum.at[g], held_accum, local.at[1]),
+        pltpu.make_async_copy(bag_rows, rows, local.at[2]),
+        pltpu.make_async_copy(bag_lengths, lengths, local.at[4]),
     ]
     for copy in held:
         copy.start()
@@ -193,17 +208,6 @@
 
     def send_raw(n):
         i, d, p, line, to = place_of(n)
-
-        @pl.when(d == 0)
-        def _():
-            for o in range(1, plane):
-                q = (p + o) % plane
-                remote(
-                    ids.at[i, :, q], raw_ids.at[i, :, p], ids_sent, ids_got.at[i],
-                    split.device(i, q, line),
-                ).start()
-            pltpu.make_async_copy(ids.at[i, :, p], raw_ids.at[i, :, p], ids_kept.at[i]).start()
-
         a = i * lines + to
         for o in range(1, plane):
             q = (p + o) % plane
@@ -220,6 +224,33 @@
     lax.fori_loop(0, ahead, first, 0)
     for copy in held:
         copy.wait()
+
+    bag = rows.shape[1]
+    for j in range(bag):
+        live = jnp.where(lengths[...] > j, rows[:, j, :], row_count) - offset
+        by_table[:, j, :] = live.astype(jnp.float32).T
+
+    def gather(step, carry):
+        i, to = step // lines, step % lines
+        for q in range(plane):
+            for kk in range(batch):
+                at = (step * plane + q) * batch + kk
+                ids[i, to, q, kk] = by_table[order[at]].astype(jnp.bfloat16)
+        return carry
+
+    lax.fori_loop(0, steps, gather, 0)
+
+    def send_ids(i, carry):
+        p, line = split.here(i, g, s)
+        for o in range(1, plane):
+            q = (p + o) % plane
+            remote(
+                ids.at[i, :, q], raw_ids.at[i, :, p], ids_sent, ids_got.at[i],
+                split.device(i, q, line),
+            ).start()
+        return carry
+
+    lax.fori_loop(0, rounds, send_ids, 0)
     others = pl.ds(0, plane - 1)
     beside = (g // split.low) * split.low + (g % split.low + 1) % split.low
     across = (g + split.low) % groups
@@ -241,7 +272,7 @@
             made_accum[pl.ds(at, 1), :] = sums
             step_size = LEARN_RATE / (jnp.sqrt(sums) + EPSILON)
             change = (total * step_size).T
-            made_weights[at] = (held_weights[at].astype(jnp.float32) - change).astype(jnp.bfloat16)
+            new_weights[g, at] = (held_weights[at].astype(jnp.float32) - change).astype(jnp.bfloat16)
             return carry
 
         lax.fori_loop(0, batch, table, 0)
@@ -252,10 +283,9 @@
             targets = [(g + o) % groups for o in range(1, groups)]
         for at, to in enumerate(targets):
             remote(
-                made_weights.at[mine], new_weights.at[g, mine],
+                new_weights.at[g, mine], new_weights.at[g, mine],
                 weights_sent, weights_got.at[i, at], (to, s),
             ).start()
-        pltpu.make_async_copy(made_weights.at[mine], new_weights.at[g, mine], local.at[2]).start()
 
     def pass_on(i):
         if not split.square:
@@ -279,8 +309,8 @@
 
         @pl.when(d == 0)
         def _():
-            wait_bytes(raw_ids.at[i, :, p], ids_kept.at[i])
             wait_bytes(raw_ids.at[i, :, others], ids_got.at[i])
+            raw_ids[i, :, p] = ids[i, :, p]
 
         wait_bytes(raw.at[a, others], raw_got.at[a])
 
@@ -318,23 +348,26 @@
                 scales.at[i, d], got_scales.at[i, d], scales_sent, scales_got.at[i, d], device
             ).start()
 
-        back = n - block - FINISH_AFTER
-        done = back // block * split.span
-
-        @pl.when((back >= 0) & (back % block < split.span))
-        def _():
-            finish(done + back % block)
-
-        later = back - PASS_AFTER
-
-        @pl.when((later >= 0) & (later % block < split.span))
-        def _():
-            pass_on(later // block * split.span + later % block)
+        for base, top, many in ((0, wide, split.span), (wide, rounds, narrow)):
+            block = many * lines
+            back = n - base * lines - block
+            ready = base + back // block * many + back % block
+
+            @pl.when((back >= 0) & (back % block < many) & (ready < top))
+            def _():
+                finish(ready)
+
+            later = back - PASS_AFTER
+            passed = base + later // block * many + later % block
+
+            @pl.when((later >= 0) & (later % block < many) & (passed < top))
+            def _():
+                pass_on(passed)
 
         return carry
 
     lax.fori_loop(0, steps, step, 0)
-    due = [i // split.span * block + block + i % split.span + FINISH_AFTER for i in range(rounds)]
+    due = [split.due(i, rounds) for i in range(rounds)]
     for i in range(rounds):
         if due[i] >= steps:
             finish(i)
@@ -359,7 +392,6 @@
     wait_bytes(raw_ids.at[:, :, others], ids_sent)
     wait_bytes(parts, parts_sent)
     wait_bytes(scales, scales_sent)
-    wait_bytes(new_weights.at[g], local.at[2])
     last.wait()
     wait_bytes(new_weights.at[pl.ds(0, groups - 1)], weights_sent)
     wait_bytes(new_accum.at[pl.ds(0, groups - 1)], accum_sent)
@@ -374,10 +406,10 @@
                 wait_bytes(new_weights.at[g, pl.ds(i * batch, batch)], weights_got.at[i, o - 1])
 
 
-def exchange(sends, ids, weights, accum, split, offset):
+def exchange(order, sends, bag_rows, bag_lengths, weights, accum, split, offset):
     steps, plane, batch, samples, width = sends.shape
     groups, quarter, row_count, _ = weights.shape
-    bag = ids.shape[-2]
+    bag = bag_rows.shape[1]
     lines = split.lines
     rounds = steps // lines
     ahead = min(STEPS_AHEAD, steps)
@@ -387,15 +419,19 @@
     anywhere = pl.BlockSpec(memory_space=pl.ANY)
     return pl.pallas_call(
         functools.partial(exchange_kernel, split, offset),
-        in_specs=[anywhere] * 4,
-        out_specs=[anywhere] * 2,
+        in_specs=[pl.BlockSpec(memory_space=pltpu.SMEM)] + [anywhere] * 5,
+        out_specs=[pl.BlockSpec(memory_space=pltpu.VMEM), anywhere],
         out_shape=[
-            jax.ShapeDtypeStruct(weights.shape, weights.dtype),
+            pltpu.VMEM(weights.shape, weights.dtype),
             jax.ShapeDtypeStruct(accum.shape, accum.dtype),
         ],
         scratch_shapes=[
             pltpu.VMEM((steps, plane, batch, samples, width), sends.dtype),
-            pltpu.VMEM((rounds, lines, plane, batch, bag, samples), ids.dtype),
+            pltpu.VMEM((rounds, lines, plane, batch, bag, samples), jnp.bfloat16),
+            pltpu.VMEM(bag_rows.shape, bag_rows.dtype),
+            pltpu.VMEM(bag_lengths.shape, bag_lengths.dtype),
+            pltpu.VMEM((bag_rows.shape[2], bag, samples), jnp.float32),
+            pltpu.VMEM((rounds, lines, plane, batch, bag, samples), jnp.bfloat16),
             pltpu.VMEM((row_count, unroll * samples), jnp.bfloat16),
             pltpu.VMEM((width, row_count), jnp.float32),
             pltpu.VMEM((rounds, far, batch, width, row_count), jnp.int16),
@@ -405,23 +441,21 @@
             pltpu.VMEM((quarter, width, row_count), jnp.float32),
             pltpu.VMEM((quarter, row_count, width), weights.dtype),
             pltpu.VMEM((quarter, row_count), jnp.float32),
-            pltpu.VMEM((quarter, row_count, width), weights.dtype),
             pltpu.VMEM((quarter, row_count), jnp.float32),
-            dma((ahead,)), dma((steps,)), dma((ahead,)), dma, dma((rounds,)), dma((rounds,)),
-            dma((4,)),
+            dma((ahead,)), dma((steps,)), dma((ahead,)), dma, dma((rounds,)),
+            dma((5,)),
             dma, dma((rounds, far)), dma, dma((rounds, far)),
             dma, dma((rounds, groups - 1)), dma((2,)), dma, dma((groups - 1,)),
         ],
         compiler_params=pltpu.CompilerParams(
-            collective_id=0, has_side_effects=True, vmem_limit_bytes=60 * 2**20
+            collective_id=0, has_side_effects=True, vmem_limit_bytes=48 * 2**20
         ),
-    )(sends, ids, weights, accum)
+    )(order, sends, bag_rows, bag_lengths, weights, accum)
 
 
 def body(grad_pooled, bag_rows, bag_lengths, table_order, weights, accum):
     held, row_count, width = weights.shape
     samples, tables, _ = grad_pooled.shape
-    bag = bag_rows.shape[2]
     split = Split(lax.axis_size("group"), lax.axis_size("shard"))
     groups, lines, plane = split.groups, split.lines, split.plane
     quarter = held // groups
@@ -440,15 +474,9 @@
     table_at = table_order[None, :] == jnp.arange(tables, dtype=jnp.int32)[:, None]
     places = jnp.sum(jnp.where(table_at, at_slot[None, :], 0), axis=1)
 
-    live = jnp.arange(bag, dtype=jnp.int32)[None, :, None] < bag_lengths[:, None, :]
-    ids = jnp.where(live, jnp.transpose(bag_rows, (0, 2, 1)), row_count) - offset
-    ids = jnp.transpose(ids.astype(jnp.float32), (2, 1, 0))
-    ids = jnp.take(ids, order, axis=0, mode="clip", unique_indices=True).astype(jnp.bfloat16)
-    ids = ids.reshape(rounds, lines, plane, batch, bag, samples)
-
     sends = arrange(grad_pooled, places).reshape(steps, plane, batch, samples, width)
     new_weights, new_accum = exchange(
-        sends, ids,
+        order, sends, jnp.transpose(bag_rows, (0, 2, 1)), bag_lengths,
         weights.reshape(groups, quarter, row_count, width),
         accum.reshape(groups, quarter, row_count),
         split, offset,

time: 286 us -> 283 us (0.990)
  local copies, waits for them, and re-layouts: 14.2 us -> 4.06 us
  Pallas kernels: 269 us -> 276 us
    pallas_call x1, Pallas kernels: 254 us -> 261 us  [exchange(): pl.pallas_call(functools.partial(exchange_kernel, split, offset), in_spec...]
    unnamed x5 -> x4, local copies, waits for them, and re-layouts: 10.8 us -> 4.06 us
where the time goes in v3:
time: 283 us
  Pallas kernels  276 us (98%)
  local copies, waits for them, and re-layouts  4.06 us (1%)
    pallas_call x1, Pallas kernels, exchange(): pl.pallas_call(functools.partial(exchange_kernel, split, offset), in_spec...  261 us
    pallas_call x1, Pallas kernels, arrange(): pl.pallas_call(arrange_kernel, grid_spec=pltpu.PrefetchScalarGridSpec(num...  15.2 us

profile of v3, /device:TPU:0, one launch (start us, length us, event | category | flops | bytes accessed | tf_op | source)
XLA Modules:
  0.0 282.7 jit_solution(11659743993573505862)
XLA Ops:
  0.6 1.9 select_reduce_fusion
  2.5 15.2 %shard_map.95 = bf16[512,128,128]{2,1,0:T(8,128)(2,1)} custom-call(s32[512]{0:T(512)} %get-tuple-element.6.place_ref, bf16[128,512,128]{2,1,0:T(8,128)(2,1)} %grad_ref.1), custom_call_target="tpu_custom_call" | custom-call | bytes 33554432 | tf_op jit(solution)/shard_map/pallas_call | solution.py:42
  17.7 260.8 %shard_map.96 = (bf16[4,16,512,128]{3,2,1,0:T(8,128)(2,1)S(1)}, f32[4,16,512]{2,1,0:T(8,128)}) custom-call(s32[512]{0:T(512)} %get-tuple-element.7.order, bf16[64,8,1,128,128]{4,3,2,1,0:T(8,128)(2,1)} %bitcast.7, s32[128,8,512]{2,1,0:T(8,128)} %bitcast.9, s32[128,512]{1,0:T(8,128)} %bag_lengths.1, bf16[4,16,512,128]{3,2,1,0:T(8,128)(2,1)} %bitcast.8, ...), custom_call_target="tpu_custom_call" | custom-call | tf_op jit(solution)/shard_map/pallas_call | solution.py:420
  278.6 0.0 copy-start
  278.6 3.4 %copy.13 = bf16[64,512,128]{2,1,0:T(8,128)(2,1)} copy(bf16[64,512,128]{2,1,0:T(8,128)(2,1)S(1)} %bitcast.6) | data formatting | bytes 16777216
  282.0 0.0 copy-done
  282.0 0.7 copy.14
Async XLA Ops:
  278.6 3.4 %copy-start = (f32[4,16,512]{2,1,0:T(8,128)S(1)}, f32[4,16,512]{2,1,0:T(8,128)}, u32[]{:S(2)}) copy-start(f32[4,16,512]{2,1,0:T(8,128)} %get-tuple-element.5) | copy-start | bytes 393220
